TPU v7x, 32 devices: a whole 2x2x4 slice. The times are simulated.
32 devices in a mesh: dp: 4 (over x, y), tp: 8 (over z, core).
Axes of the slice: x: 2, y: 2, z: 4, core: 2. Of those that a mesh axis runs over, the one named last changes fastest.
Arguments:
- hidden: bfloat16 [4, 512, 4096], P('dp', 'tp'), parts along dimension 0
- vision: bfloat16 [4, 8192, 4096], P('dp', 'tp'), parts along dimension 0
- positions: int32 [4, 512], P('dp', 'tp'), parts along dimension 0
- tile_mask: int32 [4, 512, 4], P('dp', 'tp'), parts along dimension 0
- ln1_a: bfloat16 [4096], replicated
- wq_a: bfloat16 [4096, 4096], P(None, 'tp')
- wk_a: bfloat16 [4096, 1024], P(None, 'tp')
- wv_a: bfloat16 [4096, 1024], P(None, 'tp')
- wo_a: bfloat16 [4096, 4096], P('tp')
- ln2_a: bfloat16 [4096], replicated
- wg_a: bfloat16 [4096, 14336], P(None, 'tp')
- wu_a: bfloat16 [4096, 14336], P(None, 'tp')
- wd_a: bfloat16 [14336, 4096], P('tp')
- ln1_b: bfloat16 [4096], replicated
- wq_b: bfloat16 [4096, 4096], P(None, 'tp')
- q_norm: bfloat16 [128], replicated
- wk_b: bfloat16 [4096, 1024], P(None, 'tp')
- wv_b: bfloat16 [4096, 1024], P(None, 'tp')
- k_norm: bfloat16 [128], replicated
- wo_b: bfloat16 [4096, 4096], P('tp')
- ln2_b: bfloat16 [4096], replicated
- wg_b: bfloat16 [4096, 14336], P(None, 'tp')
- wu_b: bfloat16 [4096, 14336], P(None, 'tp')
- wd_b: bfloat16 [14336, 4096], P('tp')
- xgates: float32 [2], replicated
Outputs:
- output: bfloat16 [4, 512, 4096], P('dp', 'tp'), parts along dimension 0
There are 4 independent parts. A program takes and returns all parts, laid end to end along the dimension named above; an argument that names none is the same for every part.
All inputs are finite; a program needn't handle non-finite values.
Results may differ from a plain program's by a relative error of at most 0.0167124.
Values are sent between devices in bfloat16 or wider.
A program may use at most 1 GiB of HBM per device.

v0:
```python
import math
import jax
import jax.numpy as jnp
from jax import lax
from jax.sharding import PartitionSpec as P

ROPE_THETA = 500000.0
ROPE_FACTOR = 8.0
LOW_FACTOR = 1.0
HIGH_FACTOR = 4.0
ORIG_CONTEXT = 8192.0
NORM_EPS = 1e-5
MASK_VALUE = -1e30


def rope_table(head_dim):
    low_wave = ORIG_CONTEXT / LOW_FACTOR
    high_wave = ORIG_CONTEXT / HIGH_FACTOR
    freq_list = []
    for freq_idx in range(head_dim // 2):
        base_freq = 1.0 / (ROPE_THETA ** (2.0 * freq_idx / head_dim))
        wave_len = 2.0 * math.pi / base_freq
        if wave_len > low_wave:
            freq_list.append(base_freq / ROPE_FACTOR)
        elif wave_len < high_wave:
            freq_list.append(base_freq)
        else:
            smooth = (ORIG_CONTEXT / wave_len - LOW_FACTOR) / (HIGH_FACTOR - LOW_FACTOR)
            freq_list.append((1.0 - smooth) * base_freq / ROPE_FACTOR + smooth * base_freq)
    return jnp.array(freq_list, dtype=jnp.float32)


def rms_scale(values, norm_gain):
    values = values.astype(jnp.float32)
    mean_sq = jnp.mean(values * values, axis=-1, keepdims=True)
    return values * lax.rsqrt(mean_sq + NORM_EPS) * norm_gain.astype(jnp.float32)


def rotate(values, cos_tab, sin_tab):
    half_dim = values.shape[-1] // 2
    first_half = values[..., :half_dim]
    second_half = values[..., half_dim:]
    return jnp.concatenate([first_half * cos_tab - second_half * sin_tab, second_half * cos_tab + first_half * sin_tab], axis=-1)


def self_attend(queries, key_vecs, val_vecs):
    seq_len = queries.shape[3]
    head_dim = queries.shape[4]
    scores = jnp.einsum('bgrtd,bsgd->bgrts', queries, key_vecs, preferred_element_type=jnp.float32) * (head_dim ** -0.5)
    causal = lax.broadcasted_iota(jnp.int32, (seq_len, seq_len), 0) >= lax.broadcasted_iota(jnp.int32, (seq_len, seq_len), 1)
    weights = jax.nn.softmax(jnp.where(causal, scores, MASK_VALUE), axis=-1).astype(jnp.bfloat16)
    return jnp.einsum('bgrts,bsgd->bgrtd', weights, val_vecs, preferred_element_type=jnp.float32).astype(jnp.bfloat16)


def cross_attend(queries, key_vecs, val_vecs, visible):
    batch_len, kv_groups, rep_heads, seq_len, head_dim = queries.shape
    vis_len = key_vecs.shape[1]
    tile_count = visible.shape[2]
    scores = jnp.einsum('bgrtd,bsgd->bgrts', queries, key_vecs, preferred_element_type=jnp.float32) * (head_dim ** -0.5)
    scores = scores.reshape(batch_len, kv_groups, rep_heads, seq_len, tile_count, vis_len // tile_count)
    scores = jnp.where(visible[:, None, None, :, :, None], scores, MASK_VALUE)
    weights = jax.nn.softmax(scores.reshape(batch_len, kv_groups, rep_heads, seq_len, vis_len), axis=-1).astype(jnp.bfloat16)
    return jnp.einsum('bgrts,bsgd->bgrtd', weights, val_vecs, preferred_element_type=jnp.float32).astype(jnp.bfloat16)


def gather_rows(values):
    return lax.all_gather(values, 'tp', axis=1, tiled=True)


def scatter_sum(partial):
    return lax.psum_scatter(partial, 'tp', scatter_dimension=1, tiled=True).astype(jnp.float32)


def gated_mlp(resid, norm_gain, w_gate, w_up, w_down):
    gathered = gather_rows(rms_scale(resid, norm_gain).astype(jnp.bfloat16))
    gate_proj = jnp.einsum('btd,df->btf', gathered, w_gate, preferred_element_type=jnp.float32)
    up_proj = jnp.einsum('btd,df->btf', gathered, w_up, preferred_element_type=jnp.float32)
    activated = (jax.nn.silu(gate_proj) * up_proj).astype(jnp.bfloat16)
    partial = jnp.einsum('btf,fd->btd', activated, w_down, preferred_element_type=jnp.float32).astype(jnp.bfloat16)
    return scatter_sum(partial)


def solution(mesh):
    act_spec = P('dp', 'tp', None)
    col_spec = P(None, 'tp')
    row_spec = P('tp', None)
    layer_a = (P(), col_spec, col_spec, col_spec, row_spec, P(), col_spec, col_spec, row_spec)
    layer_b = (P(), col_spec, P(), col_spec, col_spec, P(), row_spec, P(), col_spec, col_spec, row_spec, P())
    in_specs = (act_spec, act_spec, P('dp', 'tp'), act_spec) + layer_a + layer_b

    def body(hidden, vision, positions, tile_mask, ln1_a, wq_a, wk_a, wv_a, wo_a, ln2_a, wg_a, wu_a, wd_a, ln1_b, wq_b, q_norm, wk_b, wv_b, k_norm, wo_b, ln2_b, wg_b, wu_b, wd_b, xgates):
        head_dim = q_norm.shape[0]
        model_dim = hidden.shape[2]
        kv_local = wk_a.shape[1] // head_dim
        rep_heads = wq_a.shape[1] // head_dim // kv_local
        query_shape = (model_dim, kv_local, rep_heads, head_dim)
        head_shape = (model_dim, kv_local, head_dim)
        out_shape = (kv_local, rep_heads, head_dim, model_dim)
        angles = gather_rows(positions).astype(jnp.float32)[..., None] * rope_table(head_dim)
        cos_tab = jnp.cos(angles)
        sin_tab = jnp.sin(angles)
        gathered = gather_rows(rms_scale(hidden, ln1_a).astype(jnp.bfloat16))
        queries = jnp.einsum('btd,dgre->bgrte', gathered, wq_a.reshape(query_shape), preferred_element_type=jnp.float32)
        queries = rotate(queries, cos_tab[:, None, None], sin_tab[:, None, None]).astype(jnp.bfloat16)
        key_vecs = jnp.einsum('btd,dge->btge', gathered, wk_a.reshape(head_shape), preferred_element_type=jnp.float32)
        key_vecs = rotate(key_vecs, cos_tab[:, :, None], sin_tab[:, :, None]).astype(jnp.bfloat16)
        val_vecs = jnp.einsum('btd,dge->btge', gathered, wv_a.reshape(head_shape), preferred_element_type=jnp.float32).astype(jnp.bfloat16)
        context = self_attend(queries, key_vecs, val_vecs)
        partial = jnp.einsum('bgrtd,grde->bte', context, wo_a.reshape(out_shape), preferred_element_type=jnp.float32).astype(jnp.bfloat16)
        h_one = (hidden.astype(jnp.float32) + scatter_sum(partial)).astype(jnp.bfloat16)
        h_two = (h_one.astype(jnp.float32) + gated_mlp(h_one, ln2_a, wg_a, wu_a, wd_a)).astype(jnp.bfloat16)
        gathered = gather_rows(rms_scale(h_two, ln1_b).astype(jnp.bfloat16))
        queries = jnp.einsum('btd,dgre->bgrte', gathered, wq_b.reshape(query_shape), preferred_element_type=jnp.float32)
        queries = rms_scale(queries, q_norm).astype(jnp.bfloat16)
        vis_full = gather_rows(vision)
        key_vecs = jnp.einsum('bsd,dge->bsge', vis_full, wk_b.reshape(head_shape), preferred_element_type=jnp.float32)
        key_vecs = rms_scale(key_vecs, k_norm).astype(jnp.bfloat16)
        val_vecs = jnp.einsum('bsd,dge->bsge', vis_full, wv_b.reshape(head_shape), preferred_element_type=jnp.float32).astype(jnp.bfloat16)
        context = cross_attend(queries, key_vecs, val_vecs, gather_rows(tile_mask) > 0)
        partial = jnp.einsum('bgrtd,grde->bte', context, wo_b.reshape(out_shape), preferred_element_type=jnp.float32).astype(jnp.bfloat16)
        row_keep = jnp.any(tile_mask > 0, axis=-1, keepdims=True).astype(jnp.float32)
        gate_vals = jnp.tanh(xgates.astype(jnp.float32))
        h_three = (h_two.astype(jnp.float32) + gate_vals[0] * row_keep * scatter_sum(partial)).astype(jnp.bfloat16)
        mlp_out = gated_mlp(h_three, ln2_b, wg_b, wu_b, wd_b)
        return (h_three.astype(jnp.float32) + gate_vals[1] * row_keep * mlp_out).astype(jnp.bfloat16)

    return jax.shard_map(body, mesh=mesh, in_specs=in_specs, out_specs=act_spec, check_vma=False)
```

profile of v0, /device:TPU:0, one launch (start us, length us, event | category | flops | bytes accessed | tf_op | source)
XLA Modules:
  0.0 1270.4 jit_solution(13751755419757475788)
XLA Ops:
  6.5 0.8 convert_element_type.151
  7.3 1.2 fusion.68
  8.6 2.0 fusion.70
  10.6 0.0 reduce-scatter.5.cloned.1.call-start
  10.7 1.3 dynamic-slice
  12.6 0.8 bitcast_dynamic-update-slice_fusion
  13.3 10.7 all-reduce
  24.0 0.1 iota_compare_fusion
  24.1 1.2 multiply_sine_fusion.1
  25.3 34.7 %all-gather.6.cloned.1.call-done = bf16[1,512,4096]{2,1,0:T(8,128)(2,1)} async-done(((bf16[1,64,4096]{2,1,0:T(8,128)(2,1)}), bf16[1,512,4096]{2,1,0:T(8,128)(2,1)}) %all-gather.6.cloned.1.call-update) | async-done | bytes 4194320 | tf_op jit(solution)/shard_map/all_gather | solution.py:67
  60.0 6.0 fusion.35
  66.0 0.2 fusion.96
  66.2 0.2 fusion.95
  66.4 1.5 fusion.59
  67.9 0.6 fusion.108
  68.5 0.8 fusion.86
  69.3 4.0 fusion.119
  73.3 1.3 fusion.65
  74.5 8.3 fusion.19
  82.9 0.0 all-gather.8.cloned.1.call-start
  82.9 0.6 copy-done.8
  83.5 48.3 %reduce-scatter.5.cloned.1.call-done = bf16[1,64,4096]{2,1,0:T(8,128)(2,1)} async-done(((bf16[1,512,4096]{2,1,0:T(8,128)(2,1)}), bf16[1,64,4096]{2,1,0:T(8,128)(2,1)}) %reduce-scatter.5.cloned.1.call-update) | async-done | bytes 524304 | tf_op jit(solution)/shard_map/reduce_scatter | solution.py:71
  131.8 1.3 fusion.72
  133.2 1.0 fusion.74
  134.2 0.3 reduce-scatter.7.cloned.1.call-start
  134.5 45.3 %all-gather.8.cloned.1.call-done = bf16[1,512,4096]{2,1,0:T(8,128)(2,1)} async-done(((bf16[1,64,4096]{2,1,0:T(8,128)(2,1)}), bf16[1,512,4096]{2,1,0:T(8,128)(2,1)}) %all-gather.8.cloned.1.call-update) | async-done | bytes 4194320 | tf_op jit(solution)/shard_map/all_gather | solution.py:67
  179.8 14.7 %fusion.29 = f32[512,1792]{1,0:T(8,128)} fusion(bf16[4096,1792]{1,0:T(8,128)(2,1)} %param.36, bf16[1,512,4096]{2,1,0:T(8,128)(2,1)} %all-gather.8.cloned.1.call-done), kind=kOutput, calls=%fused_computation.32 | convolution fusion | flops 7516192768 | bytes 22544384 | tf_op jit(solution)/shard_map/btd,df->btf/dot_general | solution.py:76
  194.5 28.6 %fusion.17 = bf16[1,512,4096]{2,1,0:T(8,128)(2,1)} fusion(bf16[1792,4096]{1,0:T(8,128)(2,1)} %param.38, f32[512,1792]{1,0:T(8,128)} %fusion.29, bf16[4096,1792]{1,0:T(8,128)(2,1)} %param.37, bf16[1,512,4096]{2,1,0:T(8,128)(2,1)} %all-gather.8.cloned.1.call-done), kind=kOutput, calls=%fused_computation.20 | convolution fusion | flops 15039987712 | bytes 41418752 | tf_op jit(solution)/shard_map/btf,fd->btd/dot_general | solution.py:79
  223.1 0.0 all-gather.10.cloned.1.call-start
  223.2 0.6 copy-done.9
  223.8 48.3 %reduce-scatter.7.cloned.1.call-done = bf16[1,64,4096]{2,1,0:T(8,128)(2,1)} async-done(((bf16[1,512,4096]{2,1,0:T(8,128)(2,1)}), bf16[1,64,4096]{2,1,0:T(8,128)(2,1)}) %reduce-scatter.7.cloned.1.call-update) | async-done | bytes 524304 | tf_op jit(solution)/shard_map/reduce_scatter | solution.py:71
  272.1 1.3 fusion.76
  273.4 2.0 fusion.78
  275.6 0.5 all-gather.12.cloned.1.call-update
  276.2 0.1 copy.71
  276.3 15.5 %all_gather.24 = s32[1,512,4]{2,0,1:T(1,128)S(1)} all-gather(s32[1,64,4]{2,0,1:T(1,128)S(1)} %copy.71), channel_id=1, replica_groups=mesh['dp'=4,'tp'=8] {'tp'}, dimensions={1}, use_global_device_ids=true | all-gather | bytes 9216 | tf_op jit(solution)/shard_map/all_gather | solution.py:67
  291.8 0.1 copy.72
  292.0 0.2 copy.73
  292.2 2.2 broadcast_in_dim.25
  294.4 10.5 copy.86
  304.9 16.9 %all-gather.10.cloned.1.call-done = bf16[1,512,4096]{2,1,0:T(8,128)(2,1)} async-done(((bf16[1,64,4096]{2,1,0:T(8,128)(2,1)}), bf16[1,512,4096]{2,1,0:T(8,128)(2,1)}) %all-gather.10.cloned.1.call-update) | async-done | bytes 4194320 | tf_op jit(solution)/shard_map/all_gather | solution.py:67
  321.8 6.0 fusion.25
  327.8 0.1 multiply_reduce_fusion.1
  327.9 559.5 %all-gather.12.cloned.1.call-done = bf16[1,8192,4096]{2,1,0:T(8,128)(2,1)} async-done(((bf16[1,1024,4096]{2,1,0:T(8,128)(2,1)}), bf16[1,8192,4096]{2,1,0:T(8,128)(2,1)}) %all-gather.12.cloned.1.call-update) | async-done | bytes 67108880 | tf_op jit(solution)/shard_map/all_gather | solution.py:67
  887.4 30.5 %multiply_reduce_fusion = (f32[8192]{0:T(1024)S(1)}, f32[8192,128]{0,1:T(8,128)}) fusion(bf16[4096,128]{1,0:T(8,128)(2,1)S(1)} %copy-done, bf16[1,8192,4096]{2,1,0:T(8,128)(2,1)} %all-gather.12.cloned.1.call-done), kind=kOutput, calls=%fused_computation.41 | convolution fusion | flops 8592023552 | bytes 72384512 | tf_op jit(solution)/shard_map/bsd,dge->bsge/dot_general | solution.py:116
  917.9 25.6 %fusion.47 = f32[4,512,8192]{2,1,0:T(8,128)} fusion(f32[8192,128]{0,1:T(8,128)} %get-tuple-element.18, f32[128]{0:T(128)S(1)} %convert_element_type.175, f32[8192]{0:T(1024)S(1)} %add_rsqrt_fusion, f32[1,4,128,1,512]{4,2,1,3,0:T(8,128)S(1)} %bitcast.151, f32[128]{0:T(128)S(1)} %convert_element_type.172, f32[4,512]{1,0:T(4,128)S(1)} %add_rsqrt_fusion.1), kind=kOutput, calls=%fused_computation.49 | convolution fusion | flops 4298899456 | bytes 72393728 | tf_op jit(solution)/shard_map/bgrtd,bsgd->bgrts/dot_general | solution.py:59
  943.5 74.4 %fusion.120 = (f32[4,512]{1,0:T(4,128)S(1)}, f32[4,512,8192]{2,1,0:T(8,128)}) fusion(f32[4,512,8192]{2,1,0:T(8,128)} %fusion.47, pred[512,8192]{1,0:T(8,128)(4,1)} %bitcast.156), kind=kOutput, calls=%fused_computation.145 | output fusion | flops 100671488 | bytes 138420224 | tf_op jit(solution)/shard_map/sub | solution.py:62
  1017.9 25.8 %fusion.14 = bf16[8192,128,1]{1,0,2:T(8,128)(2,1)S(1)} fusion(bf16[4096,128]{1,0:T(8,128)(2,1)S(1)} %copy-done.15, bf16[1,8192,4096]{2,1,0:T(8,128)(2,1)} %all-gather.12.cloned.1.call-done), kind=kOutput, calls=%fused_computation.15 | convolution fusion | flops 8590983168 | bytes 70254592 | tf_op jit(solution)/shard_map/bsd,dge->bsge/dot_general | solution.py:118
  1043.8 23.1 %fusion.58 = bf16[4,512,128]{2,1,0:T(8,128)(2,1)S(1)} fusion(bf16[8192,128,1]{1,0,2:T(8,128)(2,1)S(1)} %fusion.14, f32[4,512,8192]{2,1,0:T(8,128)} %get-tuple-element.22, f32[4,512]{1,0:T(4,128)S(1)} %get-tuple-element.21), kind=kOutput, calls=%fused_computation.71 | convolution fusion | flops 4328783872 | bytes 69738496 | tf_op jit(solution)/shard_map/bgrts,bsgd->bgrtd/dot_general | solution.py:63
  1066.9 6.1 fusion.20
  1073.0 0.0 all-gather.14.cloned.1.call-start
  1073.0 0.6 copy-done.18
  1073.6 0.1 copy-done.10
  1073.6 0.6 fusion.118
  1074.2 1.3 broadcast_select_fusion
  1075.6 45.5 %reduce-scatter.9.cloned.1.call-done = bf16[1,64,4096]{2,1,0:T(8,128)(2,1)} async-done(((bf16[1,512,4096]{2,1,0:T(8,128)(2,1)}), bf16[1,64,4096]{2,1,0:T(8,128)(2,1)}) %reduce-scatter.9.cloned.1.call-update) | async-done | bytes 524304 | tf_op jit(solution)/shard_map/reduce_scatter | solution.py:71
  1121.1 1.5 fusion.80
  1122.5 1.0 fusion.82
  1123.5 0.0 reduce-scatter.11.cloned.1.call-start
  1123.6 45.5 %all-gather.14.cloned.1.call-done = bf16[1,512,4096]{2,1,0:T(8,128)(2,1)} async-done(((bf16[1,64,4096]{2,1,0:T(8,128)(2,1)}), bf16[1,512,4096]{2,1,0:T(8,128)(2,1)}) %all-gather.14.cloned.1.call-update) | async-done | bytes 4194320 | tf_op jit(solution)/shard_map/all_gather | solution.py:67
  1169.1 14.6 %fusion.23 = f32[512,1792]{1,0:T(8,128)} fusion(bf16[4096,1792]{1,0:T(8,128)(2,1)} %param.47, bf16[1,512,4096]{2,1,0:T(8,128)(2,1)} %all-gather.14.cloned.1.call-done), kind=kOutput, calls=%fused_computation.26 | convolution fusion | flops 7516192768 | bytes 22544384 | tf_op jit(solution)/shard_map/btd,df->btf/dot_general | solution.py:76
  1183.8 28.7 %fusion.18 = bf16[1,512,4096]{2,1,0:T(8,128)(2,1)} fusion(bf16[1792,4096]{1,0:T(8,128)(2,1)} %param.49, f32[512,1792]{1,0:T(8,128)} %fusion.23, bf16[4096,1792]{1,0:T(8,128)(2,1)} %param.48, bf16[1,512,4096]{2,1,0:T(8,128)(2,1)} %all-gather.14.cloned.1.call-done), kind=kOutput, calls=%fused_computation.21 | convolution fusion | flops 15039987712 | bytes 41418752 | tf_op jit(solution)/shard_map/btf,fd->btd/dot_general | solution.py:79
  1212.4 49.0 %reduce-scatter.11.cloned.1.call-done = bf16[1,64,4096]{2,1,0:T(8,128)(2,1)} async-done(((bf16[1,512,4096]{2,1,0:T(8,128)(2,1)}), bf16[1,64,4096]{2,1,0:T(8,128)(2,1)}) %reduce-scatter.11.cloned.1.call-update) | async-done | bytes 524304 | tf_op jit(solution)/shard_map/reduce_scatter | solution.py:71
  1261.4 2.1 fusion.83
  (61 shorter events, 0.4 us)
Async XLA Ops:
  6.5 880.9 %copy-start = (bf16[4096,128]{1,0:T(8,128)(2,1)S(1)}, bf16[4096,128]{1,0:T(8,128)(2,1)}, u32[]{:S(2)}) copy-start(bf16[4096,128]{1,0:T(8,128)(2,1)} %param.42) | copy-start | bytes 3145732
  6.5 53.5 %all-gather.6.cloned.1.call-start = ((), (), s32[]{:S(2)}) async-start(), calls=%async_computation.4 | async-start | bytes 4718592 | tf_op jit(solution)/shard_map/all_gather | solution.py:67
  10.6 121.2 %reduce-scatter.5.cloned.1.call-start = ((), (), s32[]{:S(2)}) async-start(), calls=%async_computation.5 | async-start | bytes 4718592 | tf_op jit(solution)/shard_map/reduce_scatter | solution.py:71
  25.3 41.0 %copy-start.7 = (bf16[4096,128]{1,0:T(8,128)(2,1)S(1)}, bf16[4096,128]{1,0:T(8,128)(2,1)}, u32[]{:S(2)}) copy-start(bf16[4096,128]{1,0:T(8,128)(2,1)} %param.32) | copy-start | bytes 3145732
  60.0 6.3 copy-start.4
  66.2 1.7 copy-start.13
  69.3 4.0 copy-start.14
  82.8 0.7 copy-start.8
  82.8 49.0 %copy-start.5 = (bf16[1,64,4096]{2,1,0:T(8,128)(2,1)S(1)}, bf16[1,64,4096]{2,1,0:T(8,128)(2,1)}, u32[]{:S(2)}) copy-start(bf16[1,64,4096]{2,1,0:T(8,128)(2,1)} %param.26) | copy-start | bytes 1572868
  82.9 96.9 %all-gather.8.cloned.1.call-start = ((), (), s32[]{:S(2)}) async-start(), calls=%async_computation.6 | async-start | bytes 4718592 | tf_op jit(solution)/shard_map/all_gather | solution.py:67
  133.2 140.2 %copy-start.2 = (bf16[1,64,4096]{2,1,0:T(8,128)(2,1)}, bf16[1,64,4096]{2,1,0:T(8,128)(2,1)S(1)}, u32[]{:S(2)}) copy-start(bf16[1,64,4096]{2,1,0:T(8,128)(2,1)S(1)} %get-tuple-element.8) | copy-start | bytes 1572868
  134.2 137.9 %reduce-scatter.7.cloned.1.call-start = ((), (), s32[]{:S(2)}) async-start(), calls=%async_computation.7 | async-start | bytes 4718592 | tf_op jit(solution)/shard_map/reduce_scatter | solution.py:71
  223.1 0.7 copy-start.9
  223.1 98.7 %all-gather.10.cloned.1.call-start = ((), (), s32[]{:S(2)}) async-start(), calls=%async_computation.8 | async-start | bytes 4718592 | tf_op jit(solution)/shard_map/all_gather | solution.py:67
  275.5 0.7 copy-start.16
  275.5 0.7 copy-start.17
  275.5 0.7 copy-start.11
  275.5 611.9 %all-gather.12.cloned.1.call-start = ((), (), s32[]{:S(2)}) async-start(), calls=%async_computation.9 | async-start | bytes 75497472 | tf_op jit(solution)/shard_map/all_gather | solution.py:67
  276.1 845.0 %reduce-scatter.9.cloned.1.call-start = ((), (), s32[]{:S(2)}) async-start(), calls=%async_computation.10 | async-start | bytes 4718592 | tf_op jit(solution)/shard_map/reduce_scatter | solution.py:71
  943.5 74.4 %copy-start.15 = (bf16[4096,128]{1,0:T(8,128)(2,1)S(1)}, bf16[4096,128]{1,0:T(8,128)(2,1)}, u32[]{:S(2)}) copy-start(bf16[4096,128]{1,0:T(8,128)(2,1)} %param.43) | copy-start | bytes 3145732
  1072.9 0.7 copy-start.18
  1072.9 0.7 copy-start.10
  1072.9 0.7 copy-start.12
  1072.9 48.1 %copy-start.3 = (bf16[1,64,4096]{2,1,0:T(8,128)(2,1)S(1)}, bf16[1,64,4096]{2,1,0:T(8,128)(2,1)}, u32[]{:S(2)}) copy-start(bf16[1,64,4096]{2,1,0:T(8,128)(2,1)} %copy-done.2) | copy-start | bytes 1572868
  1072.9 48.1 %copy-start.6 = (bf16[1,64,4096]{2,1,0:T(8,128)(2,1)S(1)}, bf16[1,64,4096]{2,1,0:T(8,128)(2,1)}, u32[]{:S(2)}) copy-start(bf16[1,64,4096]{2,1,0:T(8,128)(2,1)} %reduce-scatter.7.cloned.1.call-done) | copy-start | bytes 1572868
  1073.0 96.2 %all-gather.14.cloned.1.call-start = ((), (), s32[]{:S(2)}) async-start(), calls=%async_computation.11 | async-start | bytes 4718592 | tf_op jit(solution)/shard_map/all_gather | solution.py:67
  1123.5 137.9 %reduce-scatter.11.cloned.1.call-start = ((), (), s32[]{:S(2)}) async-start(), calls=%async_computation.12 | async-start | bytes 4718592 | tf_op jit(solution)/shard_map/reduce_scatter | solution.py:71
  1183.8 79.7 %copy-start.1 = (bf16[4096,128]{1,0:T(8,128)(2,1)S(1)}, bf16[4096,128]{1,0:T(8,128)(2,1)}, u32[]{:S(2)}) copy-start(bf16[4096,128]{1,0:T(8,128)(2,1)} %param.42) | copy-start | bytes 3145732
Sparse Core Ops, SparseCore 0:
  10.8 49.2 all-gather.5
  83.0 48.7 reduce-scatter.4
  134.3 45.4 all-gather.7
  223.2 48.7 reduce-scatter.6
  275.6 46.1 all-gather.9
  323.2 564.0 all-gather.11
  1073.1 47.9 reduce-scatter.8
  1123.7 45.4 all-gather.13
  1212.6 48.7 reduce-scatter.10
where the time goes:
time: 1280 us; the launch traced here: 1270 us
  waiting for transfers between devices  894 us (70%)
  matrix products  221 us (17%)
  other arithmetic  96.4 us (8%)
  blocking collectives  26.2 us (2%)
  local copies, waits for them, and re-layouts  17.7 us (1%)
  between operations  14.5 us (1%)
    all_gather x5, waiting for transfers between devices, gather_rows(): return lax.all_gather(values, 'tp', axis=1, tiled=True)  702 us
    reduce_scatter x4, waiting for transfers between devices, scatter_sum(): lax.psum_scatter(partial, 'tp', scatter_dimension=1, tiled=True)  191 us
    sub x1, other arithmetic, cross_attend(): jax.nn.softmax(scores.reshape(batch_len, kv_groups, rep_heads, seq_len, v...  74.4 us
    dot_general x2, matrix products, gated_mlp(): jnp.einsum('btf,fd->btd', activated, w_down, preferred_element_type=jnp.f...  57.2 us
    dot_general x1, matrix products, body(): jnp.einsum('bsd,dge->bsge', vis_full, wk_b.reshape(head_shape), preferred...  30.5 us
    dot_general x2, matrix products, gated_mlp(): jnp.einsum('btd,df->btf', gathered, w_gate, preferred_element_type=jnp.fl...  29.4 us
    dot_general x1, matrix products, body(): jnp.einsum('bsd,dge->bsge', vis_full, wv_b.reshape(head_shape), preferred...  25.8 us
  transfers between devices with their start and end apart: 9, of which 9 were waited for; matrix products, arithmetic and copies ran while one was open for 2% of the time, Pallas kernels for 0%

commit v1 on v0

v1 whole, which is shorter than its diff:
```python
import functools
import math
import jax
import jax.numpy as jnp
from jax import lax
from jax.experimental import pallas as pl
from jax.experimental.pallas import tpu as pltpu
from jax.sharding import PartitionSpec as P

ROPE_THETA = 500000.0
ROPE_FACTOR = 8.0
LOW_FACTOR = 1.0
HIGH_FACTOR = 4.0
ORIG_CONTEXT = 8192.0
NORM_EPS = 1e-5
MASK_VALUE = -1e30
BF16 = jnp.bfloat16
F32 = jnp.float32
MIB = 1048576
BLOCK = 256
UNROLL = 7


def rope_table(head_dim):
    low_wave = ORIG_CONTEXT / LOW_FACTOR
    high_wave = ORIG_CONTEXT / HIGH_FACTOR
    freq_list = []
    for freq_idx in range(head_dim // 2):
        base_freq = 1.0 / (ROPE_THETA ** (2.0 * freq_idx / head_dim))
        wave_len = 2.0 * math.pi / base_freq
        if wave_len > low_wave:
            freq_list.append(base_freq / ROPE_FACTOR)
        elif wave_len < high_wave:
            freq_list.append(base_freq)
        else:
            smooth = (ORIG_CONTEXT / wave_len - LOW_FACTOR) / (HIGH_FACTOR - LOW_FACTOR)
            freq_list.append((1.0 - smooth) * base_freq / ROPE_FACTOR + smooth * base_freq)
    return jnp.array(freq_list, dtype=jnp.float32)


def rms_scale(values, norm_gain):
    values = values.astype(jnp.float32)
    mean_sq = jnp.mean(values * values, axis=-1, keepdims=True)
    return values * lax.rsqrt(mean_sq + NORM_EPS) * norm_gain.astype(jnp.float32)


def rotate(values, cos_tab, sin_tab):
    half_dim = values.shape[-1] // 2
    first_half = values[..., :half_dim]
    second_half = values[..., half_dim:]
    return jnp.concatenate([first_half * cos_tab - second_half * sin_tab, second_half * cos_tab + first_half * sin_tab], axis=-1)


def self_attend(queries, key_vecs, val_vecs):
    seq_len = queries.shape[3]
    head_dim = queries.shape[4]
    scores = jnp.einsum('bgrtd,bsgd->bgrts', queries, key_vecs, preferred_element_type=jnp.float32) * (head_dim ** -0.5)
    causal = lax.broadcasted_iota(jnp.int32, (seq_len, seq_len), 0) >= lax.broadcasted_iota(jnp.int32, (seq_len, seq_len), 1)
    weights = jax.nn.softmax(jnp.where(causal, scores, MASK_VALUE), axis=-1).astype(jnp.bfloat16)
    return jnp.einsum('bgrts,bsgd->bgrtd', weights, val_vecs, preferred_element_type=jnp.float32).astype(jnp.bfloat16)


def flash_kernel(scale, q_ref, vis_ref, *refs):
    kvs, (out, s_ref, v_ref) = refs[:-3], refs[-3:]
    rows, hd = q_ref.shape
    n = kvs[0].shape[0]

    @pl.when((pl.program_id(0) == 0) & (pl.program_id(1) == 0))
    def _():
        for j, kv in enumerate(kvs):
            v_ref[j, :, :hd] = kv[:, hd:]
            v_ref[j, :, hd:] = jnp.ones((n, hd), BF16)

    q = q_ref[...]
    top = jnp.full((rows, 128), -jnp.inf, F32)
    seen = [jnp.broadcast_to(vis_ref[:, j:j + 1], (rows, 128)) > 0 for j in range(len(kvs))]
    for j, kv in enumerate(kvs):
        s = lax.dot_general(q, kv[:, :hd], (((1,), (1,)), ((), ())), preferred_element_type=F32)
        s_ref[j] = s
        best = s[:, :128]
        for k in range(1, n // 128):
            best = jnp.maximum(best, s[:, k * 128:(k + 1) * 128])
        top = jnp.where(seen[j], jnp.maximum(top, best), top)
    top = jnp.max(top, axis=-1, keepdims=True)
    acc = jnp.zeros((rows, 2 * hd), F32)
    for j in range(len(kvs)):
        shift = jnp.where(vis_ref[:, j:j + 1] > 0, top, 1e30)
        p = jnp.exp2((s_ref[j] - shift) * scale).astype(BF16)
        acc += jnp.dot(p, v_ref[j], preferred_element_type=F32)
    l = acc[:, hd:]
    out[...] = (acc[:, :hd] / jnp.where(l == 0, 1.0, l)).astype(BF16)


def flash_call(queries, seen, kvs):
    toks, width = queries.shape
    n, kw = kvs[0].shape
    hd = kw // 2
    heads = width // hd
    rows = 256
    scale = hd ** -0.5 * math.log2(math.e)
    return pl.pallas_call(
        functools.partial(flash_kernel, scale),
        grid=(toks // rows, heads),
        in_specs=[pl.BlockSpec((rows, hd), lambda i, h: (i, h)), pl.BlockSpec((rows, len(kvs)), lambda i, h: (i, 0))]
        + [pl.BlockSpec((n, kw), lambda i, h: (0, 0))] * len(kvs),
        out_specs=pl.BlockSpec((rows, hd), lambda i, h: (i, h)),
        out_shape=jax.ShapeDtypeStruct((toks, width), BF16),
        scratch_shapes=[pltpu.VMEM((len(kvs), rows, n), F32), pltpu.VMEM((len(kvs), n, kw), BF16)],
        compiler_params=pltpu.CompilerParams(vmem_limit_bytes=48 * MIB),
        cost_estimate=pl.CostEstimate(flops=4 * toks * width * n * len(kvs), bytes_accessed=8 * MIB, transcendentals=toks * heads * n * len(kvs)),
        name="cross_flash",
    )(queries, seen, *kvs)


LINE = 4
PIECES = 4
VMEM_SPEC = pl.BlockSpec(memory_space=pltpu.VMEM)
ANY_SPEC = pl.BlockSpec(memory_space=pl.ANY)
DMA = pltpu.SemaphoreType.DMA


class Roles:
    def __init__(self):
        t = lax.axis_index("tp")
        self.t = t
        self.c = lax.rem(t, 2)
        self.o = 1 - self.c
        z = lax.div(t, 2)
        self.z = z
        up_side = z < LINE // 2
        s = jnp.where(up_side, 1, -1)
        self.is_end = (z == 0) | (z == LINE - 1)
        self.is_mid = jnp.logical_not(self.is_end)
        self.sib = t + self.o - self.c
        self.ahead = t + s + s
        self.behind = t - s - s
        self.dir_a = jnp.where(up_side, 0, 1)
        self.dir_b = 1 - self.dir_a
        self.near, self.far, self.back = z + s, z + s + s, z - s
        self.last = self.far + s
        self.arrive = (self.near, jnp.where(self.is_end, self.far, self.back), jnp.where(self.is_end, self.last, self.far))

    def mid(self, fn):
        pl.when(self.is_mid)(fn)

    def end(self, fn):
        pl.when(self.is_end)(fn)

    def meet(self, others=()):
        barrier = pltpu.get_barrier_semaphore()
        for peer in (self.sib, self.ahead):
            pl.semaphore_signal(barrier, device_id={"tp": peer})
        for peer in others:
            pl.semaphore_signal(barrier, device_id={"dp": peer})
        n = len(others)

        def mid_meet():
            pl.semaphore_signal(barrier, device_id={"tp": self.behind})
            pl.semaphore_wait(barrier, n + 3)

        self.mid(mid_meet)
        self.end(lambda: pl.semaphore_wait(barrier, n + 2))


def pick(i, values):
    out = values[-1]
    for n, v in enumerate(values[:-1]):
        out = jnp.where(i == n, v, out)
    return out


def norm_rows(h_ref, gain_ref):
    return rms_scale(h_ref[:], gain_ref[:]).astype(BF16)


def landed(ref, sem):
    pltpu.make_async_copy(ref, ref, sem).wait()


class Gather:
    def __init__(self, roles, *sets):
        self.r, self.sets = roles, sets

    def copies(self, b, way, dev):
        c = self.r.c
        return [pltpu.make_async_remote_copy(
            src_ref=buf.at[b, c], dst_ref=buf.at[b, c], send_sem=send.at[way, b], recv_sem=recv.at[c, b],
            device_id={"tp": dev}) for buf, send, recv in self.sets]

    def go(self, b, way, dev):
        for cp in self.copies(b, way, dev):
            cp.start()

    def ahead(self, b):
        self.go(b, 0, self.r.ahead)

    def behind(self, b):
        self.go(b, 1, self.r.behind)

    def across(self, b):
        self.go(b, 2, self.r.sib)

    def wait(self, b, rail):
        for buf, _, recv in self.sets:
            landed(buf.at[b, rail], recv.at[rail, b])

    def ready(self, b):
        self.wait(b, self.r.o)

    def take(self, b):
        self.wait(b, self.r.c)
        self.across(b)

    def begin(self):
        z = self.r.z
        self.ahead(z)
        self.r.mid(lambda: self.behind(z))
        self.across(z)

    def first(self):
        r = self.r
        self.take(r.near)

        def more():
            self.behind(r.near)
            self.take(r.back)
            self.ahead(r.back)

        r.mid(more)

    def second(self):
        self.take(self.r.far)
        self.r.mid(lambda: self.behind(self.r.far))

    def third(self):
        self.r.end(lambda: self.take(self.r.last))

    def finish(self):
        r = self.r

        def sent(b, way, dev):
            for cp in self.copies(b, way, dev):
                cp.wait_send()

        sent(r.z, 0, r.ahead)
        for b in (r.z, *r.arrive):
            sent(b, 2, r.sib)

        def more():
            for b in (r.z, r.near, r.far):
                sent(b, 1, r.behind)
            sent(r.back, 0, r.ahead)

        r.mid(more)


class Sum:
    def __init__(self, roles, pbuf, sibr, rbuf, psend, precv, csend, crecv):
        self.r, self.pbuf, self.sibr, self.rbuf = roles, pbuf, sibr, rbuf
        self.psend, self.precv, self.csend, self.crecv = psend, precv, csend, crecv
        self.width = pbuf.shape[-1] // PIECES

    def cols(self, q):
        return pl.ds(pl.multiple_of(q * self.width, self.width), self.width)

    def pair(self, b, q):
        return pltpu.make_async_remote_copy(
            src_ref=self.pbuf.at[b, self.r.o, :, self.cols(q)], dst_ref=self.sibr.at[b, :, self.cols(q)],
            send_sem=self.psend.at[b, q], recv_sem=self.precv.at[b, q], device_id={"tp": self.r.sib})

    def chain(self, b, d, q, dev):
        return pltpu.make_async_remote_copy(
            src_ref=self.pbuf.at[b, self.r.c, :, self.cols(q)], dst_ref=self.rbuf.at[d, b, :, self.cols(q)],
            send_sem=self.csend.at[b, q], recv_sem=self.crecv.at[d, b, q], device_id={"tp": dev})

    def both(self, b, q):
        cols = self.cols(q)
        landed(self.sibr.at[b, :, cols], self.precv.at[b, q])
        return self.pbuf[b, self.r.c, :, cols].astype(F32) + self.sibr[b, :, cols].astype(F32)

    def arrived(self, d, b, q):
        ref = self.rbuf.at[d, b, :, self.cols(q)]
        landed(ref, self.crecv.at[d, b, q])
        return ref[:].astype(F32)

    def pass_on(self, b, d, q, dev, first):
        total = self.both(b, q)
        if not first:
            total = total + self.arrived(d, b, q)
        self.pbuf[b, self.r.c, :, self.cols(q)] = total.astype(BF16)
        self.chain(b, d, q, dev).start()

    def from_end(self, b):
        for q in range(PIECES):
            self.pass_on(b, self.r.dir_a, q, self.r.ahead, True)

    def relay(self, groups):
        r = self.r

        def run():
            for group in groups:
                for q in range(PIECES):
                    for b in group:
                        if b is r.back:
                            self.pass_on(b, r.dir_b, q, r.behind, False)
                        else:
                            self.pass_on(b, r.dir_a, q, r.ahead, False)

        r.mid(run)

    def finish(self, h_ref, scale_ref, out_ref):
        r = self.r
        for q in range(PIECES):
            cols = self.cols(q)
            out_ref[:, cols] = self.both(r.z, q) + self.arrived(r.dir_b, r.z, q)

            def more():
                out_ref[:, cols] += self.arrived(r.dir_a, r.z, q)

            r.mid(more)
        h_ref[:] = (h_ref[:].astype(F32) + scale_ref[:] * out_ref[:]).astype(BF16)
        for b in (r.z, *r.arrive):
            for q in range(PIECES):
                self.pair(b, q).wait_send()
        for b in r.arrive:
            for q in range(PIECES):
                self.chain(b, r.dir_a, q, r.ahead).wait_send()


def sum_scratch(rows, dim):
    two = DMA((LINE, PIECES))
    return [
        pltpu.VMEM((LINE, 2, rows, dim), BF16), pltpu.VMEM((LINE, rows, dim), BF16), pltpu.VMEM((2, LINE, rows, dim), BF16),
        two, two, two, DMA((2, LINE, PIECES)),
    ]


def gather_scratch():
    return [DMA((3, LINE)), DMA((2, LINE))]


def comm_params(cid, mib):
    return pltpu.CompilerParams(collective_id=cid, has_side_effects=True, vmem_limit_bytes=int(mib * MIB))


def silu(x):
    return x / (1.0 + jnp.exp(-x))


def mlp_kernel(h_ref, gain_ref, scale_ref, wg_hbm, wu_hbm, wd_hbm, out_ref, xbuf, wg, wu, wd, act, total, asend, arecv, wsem, *sums):
    r = Roles()
    gather = Gather(r, (xbuf, asend, arecv))
    sums = Sum(r, *sums)
    weights = ((wg_hbm, wg, wsem.at[0]), (wu_hbm, wu, wsem.at[1]), (wd_hbm, wd, wsem.at[2]))
    for src, dst, sem in weights:
        n = src.shape[0] // LINE
        for i in range(LINE):
            pltpu.make_async_copy(src.at[pl.ds(i * n, n)], dst.at[pl.ds(i * n, n)], sem).start()
    xbuf[r.z, r.c] = norm_rows(h_ref, gain_ref)
    r.meet()
    gather.begin()
    rows, dim = h_ref.shape

    def compute(b):
        x = xbuf[b].reshape(2 * rows, dim)

        def inner(f, carry):
            cols = pl.ds(pl.multiple_of(f * BLOCK, BLOCK), BLOCK)
            g = jnp.dot(x, wg[:, cols], preferred_element_type=F32)
            u = jnp.dot(x, wu[:, cols], preferred_element_type=F32)
            act[:, cols] = (silu(g) * u).astype(BF16)
            return carry

        lax.fori_loop(0, act.shape[1] // BLOCK, inner, 0, unroll=UNROLL)

        def outer(q, carry):
            p = jnp.dot(act[:], wd[:, sums.cols(q)], preferred_element_type=F32).astype(BF16)
            sums.pbuf[b, :, :, sums.cols(q)] = p.reshape(2, rows, sums.width)
            sums.pair(b, q).start()
            return carry

        lax.fori_loop(0, PIECES, outer, 0)

    def step(i, carry):
        @pl.when(i == 0)
        def _():
            gather.first()
            for src, dst, sem in weights:
                pltpu.make_async_copy(src, dst, sem).wait()

        pl.when(i == 1)(gather.second)
        pl.when(i == 2)(gather.third)
        pl.when(i == 3)(lambda: sums.relay(((r.near,),)))
        b = pick(i, (*r.arrive, r.z))
        gather.ready(b)
        compute(b)
        pl.when(r.is_end & (i < 3))(lambda: sums.from_end(b))
        return carry

    lax.fori_loop(0, LINE, step, 0)
    sums.relay(((r.far, r.back),))
    out_ref[:] = h_ref[:]
    sums.finish(out_ref, scale_ref, total)
    gather.finish()


def mlp_call(h, gain, scale, w_gate, w_up, w_down, cid):
    rows, dim = h.shape
    ff = w_gate.shape[1]
    return pl.pallas_call(
        mlp_kernel,
        in_specs=[VMEM_SPEC] * 3 + [ANY_SPEC] * 3,
        out_specs=VMEM_SPEC,
        out_shape=jax.ShapeDtypeStruct((rows, dim), BF16),
        scratch_shapes=[
            pltpu.VMEM((LINE, 2, rows, dim), BF16),
            pltpu.VMEM((dim, ff), BF16), pltpu.VMEM((dim, ff), BF16), pltpu.VMEM((ff, dim), BF16),
            pltpu.VMEM((2 * rows, ff), BF16), pltpu.VMEM((rows, dim), F32),
        ] + gather_scratch() + [DMA((3,))] + sum_scratch(rows, dim),
        compiler_params=comm_params(cid, 63.9),
        cost_estimate=pl.CostEstimate(flops=48 * rows * dim * ff, bytes_accessed=6 * dim * ff, transcendentals=0),
    )(h, gain[None], scale, w_gate, w_up, w_down)


def start_kernel(h_ref, gain_ref, small_ref, w_ref, kgain_ref, wq_hbm, wk_hbm, wv_hbm, vis_hbm, q_out, k_out, v_out, small_out, *rest):
    kv_outs, rest = rest[:2 * LINE], rest[2 * LINE:]
    w_all, acc, vis, wq, wk, wv, xbuf, xsend, xrecv, isend, irecv, lsem, zsend, zrecv, ysend, yrecv, hsend, hrecv, dsend, drecv, ssend, srecv = rest
    r = Roles()
    z, c, t, s_near, s_far = r.z, r.c, r.t, r.near, r.far
    b0, b1, b2 = r.arrive
    d = lax.axis_index("dp")
    dd = w_all.shape[0] - 1 - d
    dy = d + 1 - 2 * lax.rem(d, 2)
    dx = w_all.shape[0] - 1 - dy
    gather = Gather(r, (xbuf, xsend, xrecv), (small_out, isend, irecv))

    xbuf[z, c] = norm_rows(h_ref, gain_ref)
    small_out[z, c] = small_ref[:]
    local = [pltpu.make_async_copy(src, dst, lsem.at[i]) for i, (src, dst) in enumerate(
        ((vis_hbm, vis), (wq_hbm, wq), (wk_hbm, wk), (wv_hbm, wv)))]
    for cp in local:
        cp.start()
    r.meet((dy, dx))

    def piece(q, b):
        return w_all.at[q, 2 * b + c]

    def send(q, b, ssem, rsem, peer, src=None):
        return pltpu.make_async_remote_copy(
            src_ref=piece(q, b) if src is None else src, dst_ref=piece(q, b), send_sem=ssem, recv_sem=rsem, device_id=peer)

    def ahead(b, src=None):
        return send(d, b, zsend.at[0, b], zrecv.at[b], {"tp": r.ahead}, src)

    def behind(b, src=None):
        return send(d, b, zsend.at[1, b], zrecv.at[b], {"tp": r.behind}, src)

    def plane(b, src=None):
        return [send(d, b, ysend.at[b], yrecv.at[b], {"dp": dy}, src), send(d, b, hsend.at[b], hrecv.at[b], {"dp": dx}, src)]

    def diag(b, q, peer):
        return send(q, b, dsend.at[b], drecv.at[b], {"dp": peer})

    def across(b, q, k, src=None):
        return send(q, b, ssend.at[k, b], srecv.at[k, b], {"tp": r.sib}, src)

    def spread(b, src=None):
        for cp in plane(b, src):
            cp.start()
        across(b, d, 0, src).start()

    def z_arrived(b):
        landed(piece(d, b), zrecv.at[b])

    def plane_arrived(b):
        even = lax.rem(b, 2) == 0
        landed(piece(dy, b), yrecv.at[b])
        pl.when(even)(lambda: diag(b, dy, dx).start())
        across(b, dy, 1).start()
        landed(piece(dx, b), hrecv.at[b])
        pl.when(jnp.logical_not(even))(lambda: diag(b, dx, dy).start())
        across(b, dx, 2).start()

    def diag_arrived(b):
        landed(piece(dd, b), drecv.at[b])
        across(b, dd, 3).start()

    rows, dim = h_ref.shape
    quarter = w_ref.shape[0]

    def kv_add(*pieces):
        for k, q, b in pieces:
            landed(w_all.at[q, 2 * b + r.o], srecv.at[k, b])

        def one(i, carry):
            n = lax.div(i, 2)
            q = pick(n, [p[1] for p in pieces])
            head = 2 * pick(n, [p[2] for p in pieces]) + lax.rem(i, 2)
            acc[head] += jnp.dot(vis[:, pl.ds(pl.multiple_of(q * quarter, quarter), quarter)], w_all[q, head], preferred_element_type=F32)
            return carry

        lax.fori_loop(0, 2 * len(pieces), one, 0)

    def products(*blocks):
        def one(i, carry):
            b = pick(i, blocks)
            x = xbuf[b].reshape(2 * rows, dim)
            at = pl.ds(pl.multiple_of(b * 2 * rows, 2 * rows), 2 * rows)
            for w, out in ((wq, q_out), (wk, k_out), (wv, v_out)):
                out[at, :] = jnp.dot(x, w[:], preferred_element_type=F32)
            return carry

        lax.fori_loop(0, len(blocks), one, 0)

    ahead(z, w_ref).start()
    r.mid(lambda: behind(z, w_ref).start())
    spread(z, w_ref)
    w_all[d, t] = w_ref[:]

    def clear(i, carry):
        acc[i] = jnp.zeros(acc.shape[1:], F32)
        return carry

    lax.fori_loop(0, 2 * LINE, clear, 0)
    for cp in local:
        cp.wait()

    z_arrived(b0)

    def more():
        behind(b0).start()
        z_arrived(r.back)
        ahead(r.back).start()

    r.mid(more)
    gather.begin()
    spread(b0)
    r.mid(lambda: spread(r.back))
    plane_arrived(z)
    z_arrived(s_far)
    r.mid(lambda: behind(s_far).start())
    spread(s_far)
    plane_arrived(b0)
    gather.first()

    def end_more():
        z_arrived(r.last)
        spread(r.last)

    r.end(end_more)
    plane_arrived(b1)
    kv_add((0, d, z), (0, d, b0), (1, dy, z), (2, dx, z))
    gather.second()
    kv_add((0, d, b1), (1, dy, b0), (2, dx, b0))
    plane_arrived(b2)
    kv_add((0, d, b2), (1, dy, b1), (2, dx, b1))
    diag_arrived(z)
    diag_arrived(b0)
    kv_add((1, dy, b2), (2, dx, b2), (3, dd, z), (3, dd, b0))
    gather.third()
    for b in (z, b0, b1, b2):
        gather.ready(b)
    products(z, b0, b1, b2)
    diag_arrived(b1)
    diag_arrived(b2)
    kv_add((3, dd, b1), (3, dd, b2))
    hd = kgain_ref.shape[1]
    for j, out in enumerate(kv_outs):
        head = lax.rem(t + j, 2 * LINE)

        def store(i, carry):
            at = pl.ds(pl.multiple_of(i * 2 * rows, 2 * rows), 2 * rows)
            out[at, :hd] = rms_scale(acc[head, at, :hd], kgain_ref[:]).astype(BF16)
            out[at, hd:] = acc[head, at, hd:].astype(BF16)
            return carry

        lax.fori_loop(0, out.shape[0] // (2 * rows), store, 0)

    for b in (z, b0, b1, b2):
        for k, q in enumerate((d, dy, dx, dd)):
            across(b, q, k).wait_send()
        for cp in plane(b):
            cp.wait_send()
        diag(b, dy, dx).wait_send()
    gather.finish()
    ahead(z).wait_send()

    def mid_sent():
        for b in (z, s_near, s_far):
            behind(b).wait_send()
        ahead(r.back).wait_send()

    r.mid(mid_sent)


def start_call(h, gain, small, w_loc, kgain, wq, wk, wv, vision, ndp, cid):
    rows, dim = h.shape
    heads = 2 * LINE
    toks = rows * heads
    quarter, width = w_loc.shape
    vtoks = vision.shape[0]
    line, four = DMA((LINE,)), DMA((4, LINE))
    return pl.pallas_call(
        start_kernel,
        in_specs=[VMEM_SPEC] * 5 + [ANY_SPEC] * 4,
        out_specs=[VMEM_SPEC] * (4 + heads),
        out_shape=[jax.ShapeDtypeStruct((toks, w.shape[1]), F32) for w in (wq, wk, wv)]
        + [jax.ShapeDtypeStruct((LINE, 2) + small.shape, jnp.int32)]
        + [jax.ShapeDtypeStruct((vtoks, width), BF16)] * heads,
        scratch_shapes=[
            pltpu.VMEM((ndp, heads, quarter, width), BF16),
            pltpu.VMEM((heads, vtoks, width), F32),
        ] + [pltpu.VMEM(w.shape, BF16) for w in (vision, wq, wk, wv)]
        + [pltpu.VMEM((LINE, 2, rows, dim), BF16)] + gather_scratch() + gather_scratch()
        + [DMA((4,)), DMA((2, LINE)), line, line, line, line, line, line, line, four, four],
        compiler_params=comm_params(cid, 60),
        cost_estimate=pl.CostEstimate(flops=toks * dim * wq.shape[1], bytes_accessed=30 * MIB, transcendentals=0),
        name="start",
    )(h, gain[None], small, w_loc, kgain[None], wq, wk, wv, vision)


def query_kernel(h_ref, gain_ref, hgain_ref, wq_hbm, out_ref, xbuf, wq, wsem, asend, arecv):
    load = pltpu.make_async_copy(wq_hbm, wq, wsem.at[0])
    load.start()
    r = Roles()
    gather = Gather(r, (xbuf, asend, arecv))
    rows, dim = h_ref.shape
    hd = hgain_ref.shape[1]
    xbuf[r.z, r.c] = norm_rows(h_ref, gain_ref)
    r.meet()
    gather.begin()
    load.wait()

    def step(i, carry):
        pl.when(i == 1)(gather.first)
        pl.when(i == 2)(gather.second)
        pl.when(i == 3)(gather.third)
        b = pick(i, (r.z, *r.arrive))
        gather.ready(b)
        y = jnp.dot(xbuf[b].reshape(2 * rows, dim), wq[:], preferred_element_type=F32)
        at = pl.ds(pl.multiple_of(b * 2 * rows, 2 * rows), 2 * rows)
        for n in range(y.shape[1] // hd):
            cols = slice(n * hd, n * hd + hd)
            out_ref[at, cols] = rms_scale(y[:, cols], hgain_ref[:]).astype(BF16)
        return carry

    lax.fori_loop(0, LINE, step, 0)
    gather.finish()


def query_call(h, gain, hgain, wq, cid):
    rows, dim = h.shape
    toks = rows * 2 * LINE
    return pl.pallas_call(
        query_kernel,
        in_specs=[VMEM_SPEC] * 3 + [ANY_SPEC],
        out_specs=VMEM_SPEC,
        out_shape=jax.ShapeDtypeStruct((toks, wq.shape[1]), BF16),
        scratch_shapes=[pltpu.VMEM((LINE, 2, rows, dim), BF16), pltpu.VMEM(wq.shape, BF16), DMA((1,))] + gather_scratch(),
        compiler_params=comm_params(cid, 24),
        cost_estimate=pl.CostEstimate(flops=2 * toks * dim * wq.shape[1], bytes_accessed=10 * MIB, transcendentals=0),
        name="query",
    )(h, gain[None], hgain[None], wq)


def output_kernel(h_ref, scale_ref, ctx, wo_hbm, out_ref, wo, wsem, total, *sums):
    load = pltpu.make_async_copy(wo_hbm, wo, wsem.at[0])
    load.start()
    r = Roles()
    sums = Sum(r, *sums)
    rows = h_ref.shape[0]
    r.meet()
    load.wait()
    order = (jnp.where(r.is_end, r.last, r.far), jnp.where(r.is_end, r.far, r.near), jnp.where(r.is_end, r.near, r.back), r.z)

    def step(i, carry):
        b = pick(i, order)
        x = ctx[pl.ds(pl.multiple_of(b * 2 * rows, 2 * rows), 2 * rows), :]

        def outer(q, carry):
            p = jnp.dot(x, wo[:, sums.cols(q)], preferred_element_type=F32).astype(BF16)
            sums.pbuf[b, :, :, sums.cols(q)] = p.reshape(2, rows, sums.width)
            sums.pair(b, q).start()
            return carry

        lax.fori_loop(0, PIECES, outer, 0)
        pl.when(r.is_end & (i < 3))(lambda: sums.from_end(b))
        return carry

    lax.fori_loop(0, LINE, step, 0)
    sums.relay(((r.far, r.back), (r.near,)))
    out_ref[:] = h_ref[:]
    sums.finish(out_ref, scale_ref, total)


def output_call(h, scale, ctx, wo, cid):
    rows, dim = h.shape
    return pl.pallas_call(
        output_kernel,
        in_specs=[VMEM_SPEC] * 3 + [ANY_SPEC],
        out_specs=VMEM_SPEC,
        out_shape=jax.ShapeDtypeStruct((rows, dim), BF16),
        scratch_shapes=[pltpu.VMEM(wo.shape, BF16), DMA((1,)), pltpu.VMEM((rows, dim), F32)] + sum_scratch(rows, dim),
        compiler_params=comm_params(cid, 32),
        cost_estimate=pl.CostEstimate(flops=2 * rows * dim * wo.shape[0], bytes_accessed=10 * MIB, transcendentals=0),
        name="output",
    )(h, scale, ctx, wo)


def solution(mesh):
    act_spec = P('dp', 'tp', None)
    col_spec = P(None, 'tp')
    row_spec = P('tp', None)
    layer_a = (P(), col_spec, col_spec, col_spec, row_spec, P(), col_spec, col_spec, row_spec)
    layer_b = (P(), col_spec, P(), col_spec, col_spec, P(), row_spec, P(), col_spec, col_spec, row_spec, P())
    in_specs = (act_spec, act_spec, P('dp', 'tp'), act_spec) + layer_a + layer_b
    ndp, ntp = mesh.shape['dp'], mesh.shape['tp']

    def perm(fn):
        pairs = []
        for d in range(ndp):
            for t in range(ntp):
                d2, t2 = fn(d, t)
                pairs.append((d * ntp + t, d2 * ntp + t2))
        return pairs

    def permute(x, fn):
        return lax.ppermute(x, ('dp', 'tp'), perm(fn))

    def body(hidden, vision, positions, tile_mask, ln1_a, wq_a, wk_a, wv_a, wo_a, ln2_a, wg_a, wu_a, wd_a, ln1_b, wq_b, q_norm, wk_b, wv_b, k_norm, wo_b, ln2_b, wg_b, wu_b, wd_b, xgates):
        dp = lax.axis_index('dp')
        tp = lax.axis_index('tp')
        head_dim = q_norm.shape[0]
        model_dim = hidden.shape[2]
        toks_local = hidden.shape[1]
        kv_local = wk_a.shape[1] // head_dim
        rep_heads = wq_a.shape[1] // head_dim // kv_local

        quarter = model_dim // ndp
        w_loc = jnp.concatenate([lax.dynamic_slice_in_dim(wk_b, dp * quarter, quarter, 0), lax.dynamic_slice_in_dim(wv_b, dp * quarter, quarter, 0)], axis=1)
        small = jnp.concatenate([positions[0][None], tile_mask[0].T, jnp.zeros((3, toks_local), jnp.int32)], axis=0)
        small = jnp.pad(small, ((0, 0), (0, 128 - toks_local)))
        queries, key_vecs, val_vecs, small, *kvs = start_call(hidden[0], ln1_a, small, w_loc, k_norm, wq_a, wk_a, wv_a, vision[0], ndp, 3)
        small = jnp.transpose(small.reshape(ntp, 8, 128)[:, :, :toks_local], (1, 0, 2)).reshape(8, ntp * toks_local)
        pos_all = small[0]
        mask_all = small[1:5]
        for j in range(1, ntp):
            kvs[j] = permute(kvs[j], lambda d, t, j=j: (d, (t + j) % ntp))

        angles = pos_all.astype(jnp.float32)[None, :, None] * rope_table(head_dim)
        cos_tab = jnp.cos(angles)
        sin_tab = jnp.sin(angles)
        queries = queries.reshape(1, -1, kv_local, rep_heads, head_dim).transpose(0, 2, 3, 1, 4)
        queries = rotate(queries, cos_tab[:, None, None], sin_tab[:, None, None]).astype(jnp.bfloat16)
        key_vecs = key_vecs.reshape(1, -1, kv_local, head_dim)
        key_vecs = rotate(key_vecs, cos_tab[:, :, None], sin_tab[:, :, None]).astype(jnp.bfloat16)
        val_vecs = val_vecs.reshape(1, -1, kv_local, head_dim).astype(jnp.bfloat16)
        context = self_attend(queries, key_vecs, val_vecs)
        context = context[0].transpose(2, 0, 1, 3).reshape(-1, wo_a.shape[0])
        ones = jnp.ones((toks_local, 1), F32)
        h_one = output_call(hidden[0], ones, context, wo_a, 6)
        h_two = mlp_call(h_one, ln2_a, ones, wg_a, wu_a, wd_a, 1)

        queries = query_call(h_two, ln1_b, q_norm, wq_b, 4)
        tiles = jnp.stack([((tp - j + ntp) % ntp) // (ntp // 4) for j in range(ntp)])
        seen = (jnp.take(mask_all, tiles, axis=0) > 0).astype(F32).T
        context = flash_call(queries, seen, kvs)
        row_keep = jnp.any(tile_mask > 0, axis=-1, keepdims=True).astype(jnp.float32)
        gate_vals = jnp.tanh(xgates.astype(jnp.float32))
        h_three = output_call(h_two, gate_vals[0] * row_keep[0], context, wo_b, 5)
        return mlp_call(h_three, ln2_b, gate_vals[1] * row_keep[0], wg_b, wu_b, wd_b, 2)[None]

    return jax.shard_map(body, mesh=mesh, in_specs=in_specs, out_specs=act_spec, check_vma=False)
```

time: 1280 us -> 520 us (0.41)
  waiting for transfers between devices: 894 us -> 0.02 us
  Pallas kernels: 0 us -> 479 us
  matrix products: 221 us -> 1.55 us
  other arithmetic: 96.4 us -> 8.92 us
  blocking collectives: 26.2 us -> 0 us
  between operations: 14.5 us -> 0.55 us
    all_gather x5 -> x0, waiting for transfers between devices: 702 us -> none  [gather_rows(): return lax.all_gather(values, 'tp', axis=1, tiled=True)]
    pallas_call x0 -> x7, Pallas kernels: none -> 479 us  [the longest x2 170 us: mlp_call(): pl.pallas_call(mlp_kernel, in_specs=[VMEM_SPEC] * 3 + [ANY_SPEC] * 3, out...]
    dot_general x12 -> x1, matrix products: 209 us -> 0.75 us  [self_attend(): jnp.einsum('bgrts,bsgd->bgrtd', weights, val_vecs, preferred_element_type...]
    reduce_scatter x4 -> x0, waiting for transfers between devices: 191 us -> none  [scatter_sum(): lax.psum_scatter(partial, 'tp', scatter_dimension=1, tiled=True)]
    sub x1 -> x0, other arithmetic: 74.4 us -> none  [cross_attend(): jax.nn.softmax(scores.reshape(batch_len, kv_groups, rep_heads, seq_len, v...]
    all_gather x1 -> x0, blocking collectives: 15.5 us -> none  [gather_rows(): return lax.all_gather(values, 'tp', axis=1, tiled=True)]
  transfers between devices with their start and end apart: 9 -> 7, of which waited for: 9 -> 0; matrix products, arithmetic and copies ran while one was open for 2% -> 3% of each run, Pallas kernels for 0% -> 41%
where the time goes in v1:
time: 520 us
  Pallas kernels  479 us (92%)
  local copies, waits for them, and re-layouts  20.3 us (4%)
  starting transfers between devices  9.42 us (2%)
  other arithmetic  8.92 us (2%)
    pallas_call x2, Pallas kernels, mlp_call(): pl.pallas_call(mlp_kernel, in_specs=[VMEM_SPEC] * 3 + [ANY_SPEC] * 3, out...  170 us
    pallas_call x2, Pallas kernels, output_call(): pl.pallas_call(output_kernel, in_specs=[VMEM_SPEC] * 3 + [ANY_SPEC], out_...  116 us
    pallas_call x1, Pallas kernels, start_call(): pl.pallas_call(start_kernel, in_specs=[VMEM_SPEC] * 5 + [ANY_SPEC] * 4, o...  103 us
    pallas_call x1, Pallas kernels, query_call(): pl.pallas_call(query_kernel, in_specs=[VMEM_SPEC] * 3 + [ANY_SPEC], out_s...  47.8 us
    pallas_call x1, Pallas kernels, flash_call(): pl.pallas_call(functools.partial(flash_kernel, scale), grid=(toks // rows...  41.4 us
  transfers between devices with their start and end apart: 7, of which 0 were waited for; matrix products, arithmetic and copies ran while one was open for 3% of the time, Pallas kernels for 41%

profile of v1, /device:TPU:0, one launch (start us, length us, event | category | flops | bytes accessed | tf_op | source)
XLA Modules:
  0.0 519.6 jit_solution(15199166534481450745)
XLA Ops:
  0.0 1.3 broadcast_in_dim.56.gain_ref
  1.3 0.1 pad.13.clone
  1.4 0.8 add_add_fusion
  2.1 0.6 pad.4.small_ref
  2.7 1.1 constant_dynamic-slice_fusion
  3.8 0.9 pad_maximum_fusion.w_ref
  4.7 103.4 %start.1 = (f32[512,512]{1,0:T(8,128)}, f32[512,128]{1,0:T(8,128)}, f32[512,128]{1,0:T(8,128)}, s32[4,2,8,128]{3,2,1,0:T(8,128)}, bf16[1024,256]{1,0:T(8,128)(2,...) custom-call(bf16[64,4096]{1,0:T(8,128)(2,1)} %bitcast.59, ...), custom_call_target="tpu_custom_call" | custom-call | flops 1073741824 | bytes 31457280 | tf_op jit(solution)/shard_map/start/pallas_call | solution.py:603
  108.1 0.0 copy-start.16
  108.1 1.9 collective-permute-start
  110.1 0.0 collective-permute-start.1
  110.1 0.0 collective-permute-start.2
  110.1 3.8 collective-permute-start.3
  113.9 0.5 collective-permute-start.4
  114.4 0.1 iota_compare_fusion
  114.5 0.5 compare_reduce_fusion
  115.0 1.6 reshape.606
  116.6 0.1 copy.51
  116.7 0.6 copy-done.12
  117.3 0.1 convert_element_type.45
  117.4 1.0 multiply_cosine_fusion.1
  118.4 1.2 fusion.26
  119.6 0.4 fusion.7
  120.0 0.8 fusion.9
  120.9 2.1 fusion.34
  123.0 0.0 copy-start.14
  123.0 0.0 copy-start.18
  123.0 0.0 copy-start.2
  123.0 0.7 fusion.6
  123.8 0.2 copy.49.ctx
  124.0 0.6 broadcast_in_dim.60.gain_ref
  124.6 0.7 fusion.33
  125.3 2.2 copy-done
  127.5 77.7 %output.2.h_ref = bf16[64,4096]{1,0:T(8,128)(2,1)S(1)} custom-call(bf16[64,4096]{1,0:T(8,128)(2,1)S(1)} %bitcast.60, f32[64,1]{1,0:T(8,128)S(1)} %broadcast_in_dim.54.scale_ref, bf16[512,512]{1,0:T(8,128)(2,1)S(1)} %copy.49.ctx, bf16[512,4096]{1,0:T(8,128)(2,1)S(1)} %copy-done), custom_call_target="tpu_custom_call" | custom-call | flops 268435456 | bytes 10485760 | tf_op jit(solution)/shard_map/output/pallas_call | solution.py:698
  205.2 0.0 copy-start.6
  205.2 0.8 copy-done.6
  206.0 89.4 %shard_map.244.h_ref = bf16[64,4096]{1,0:T(8,128)(2,1)} custom-call(bf16[64,4096]{1,0:T(8,128)(2,1)} %copy-done.6, bf16[1,4096]{1,0:T(2,128)(2,1)} %broadcast_in_dim.60.gain_ref, f32[64,1]{1,0:T(8,128)} %copy-done.7, bf16[4096,1792]{1,0:T(8,128)(2,1)} %wg_hbm.2, bf16[4096,1792]{1,0:T(8,128)(2,1)} %wu_hbm.2, bf16[1792,4096]{1,0:T(8,128)(2,1)} %wd_hbm.2), custom_call_target="tpu_custom_call" | custom-call | flops 22548578304 | bytes 44040192 | tf_op jit(solution)/shard_map/pallas_call | solution.py:410
  295.5 1.8 select_bitcast_fusion
  297.3 0.8 slice.49
  298.0 0.1 copy.44.scale_ref
  298.1 0.7 broadcast_in_dim.61.gain_ref
  298.9 0.1 slice.39
  299.1 0.1 stack.62
  299.2 0.1 stack.53
  299.3 0.0 collective-permute-done.refs_1_
  299.3 3.2 collective-permute-start.5
  302.5 0.0 collective-permute-done.1.refs_2_
  302.5 0.6 gather_fusion
  303.1 0.1 fusion.27
  303.2 0.1 copy.43
  303.3 1.3 broadcast_in_dim.65.gain_ref
  304.6 0.7 copy.45.scale_ref
  305.3 1.0 copy-done.3
  306.4 2.2 copy-done.8
  308.5 47.8 %query.1.q_ref = bf16[512,512]{1,0:T(8,128)(2,1)S(1)} custom-call(bf16[64,4096]{1,0:T(8,128)(2,1)S(1)} %copy-done.3, bf16[1,4096]{1,0:T(2,128)(2,1)S(1)} %broadcast_in_dim.61.gain_ref, bf16[1,128]{1,0:T(2,128)(2,1)S(1)} %bitcast.62, bf16[4096,512]{1,0:T(8,128)(2,1)S(1)} %copy-done.8), custom_call_target="tpu_custom_call" | custom-call | flops 2147483648 | bytes 10485760 | tf_op jit(solution)/shard_map/query/pallas_call | solution.py:654
  356.3 0.0 collective-permute-done.3.refs_4_
  356.4 0.0 collective-permute-done.4.refs_5_
  356.4 0.0 collective-permute-done.6.refs_7_
  356.4 0.0 copy-start.1
  356.4 41.4 %cross_flash.1.ctx = bf16[512,512]{1,0:T(8,128)(2,1)S(1)} custom-call(bf16[512,512]{1,0:T(8,128)(2,1)S(1)} %query.1.q_ref, f32[512,8]{1,0:T(8,128)S(1)} %bitcast.61, bf16[1024,256]{1,0:T(8,128)(2,1)S(1)} %copy-done.9, bf16[1024,256]{1,0:T(8,128)(2,1)} %collective-permute-done.refs_1_, bf16[1024,256]{1,0:T(8,128)(2,1)} %collective-permute-done.1.refs_2_, ...), custom_call_target="tpu_custom_call" | custom-call | flops 8589934592 | bytes 8388608 | tf_op jit(solution)/shard_map/cross_flash/pallas_call | solution.py:101
  397.8 38.2 %output.3.h_ref = bf16[64,4096]{1,0:T(8,128)(2,1)S(1)} custom-call(bf16[64,4096]{1,0:T(8,128)(2,1)S(1)} %copy-done.4, f32[64,1]{1,0:T(8,128)S(1)} %copy.44.scale_ref, bf16[512,512]{1,0:T(8,128)(2,1)S(1)} %cross_flash.1.ctx, bf16[512,4096]{1,0:T(8,128)(2,1)S(1)} %copy-done.1), custom_call_target="tpu_custom_call" | custom-call | flops 268435456 | bytes 10485760 | tf_op jit(solution)/shard_map/output/pallas_call | solution.py:698
  436.0 0.0 copy-start.5
  436.0 0.8 copy-done.5
  436.8 81.0 %shard_map.245 = bf16[64,4096]{1,0:T(8,128)(2,1)} custom-call(bf16[64,4096]{1,0:T(8,128)(2,1)} %copy-done.5, bf16[1,4096]{1,0:T(2,128)(2,1)} %broadcast_in_dim.65.gain_ref, f32[64,1]{1,0:T(8,128)} %copy.45.scale_ref, bf16[4096,1792]{1,0:T(8,128)(2,1)} %wg_hbm.3, bf16[4096,1792]{1,0:T(8,128)(2,1)} %wu_hbm.3, bf16[1792,4096]{1,0:T(8,128)(2,1)} %wd_hbm.3), custom_call_target="tpu_custom_call" | custom-call | flops 22548578304 | bytes 44040192 | tf_op jit(solution)/shard_map/pallas_call | solution.py:410
  517.8 1.9 copy.53
  (37 shorter events, 0.1 us)
Async XLA Ops:
  4.7 109.8 %copy-start.15 = (s32[1,64,4]{1,2,0:T(4,128)S(1)}, s32[1,64,4]{1,2,0:T(4,128)}, u32[]{:S(2)}) copy-start(s32[1,64,4]{1,2,0:T(4,128)} %param.29) | copy-start | bytes 3076
  108.1 8.5 %copy-start.13 = (s32[4,2,8,128]{3,2,1,0:T(8,128)S(1)}, s32[4,2,8,128]{3,2,1,0:T(8,128)}, u32[]{:S(2)}) copy-start(s32[4,2,8,128]{3,2,1,0:T(8,128)} %get-tuple-element.18) | copy-start | bytes 98308
  108.1 9.2 %copy-start.16 = (f32[64]{0:T(128)S(1)}, f32[64]{0:T(128)}, u32[]{:S(2)}) copy-start(f32[64]{0:T(128)} %constant.174.clone) | copy-start | bytes 772
  108.1 10.2 %copy-start.11 = (f32[512,128]{1,0:T(8,128)S(1)}, f32[512,128]{1,0:T(8,128)}, u32[]{:S(2)}) copy-start(f32[512,128]{1,0:T(8,128)} %get-tuple-element.19) | copy-start | bytes 786436
  108.1 191.1 %collective-permute-start = (bf16[1024,256]{1,0:T(8,128)(2,1)}, bf16[1024,256]{1,0:T(8,128)(2,1)}, u32[]{:S(2)}, u32[]{:S(2)}) collective-permute-start(bf16[1024,256]{1,0:T(8,128)(2,1)} %get-tuple-element.22), channel_id=1, source_target_pairs={{0,1},{1,2},{2,3},{3,4},{4,5},{5,6},{6,7},{7,0},{8,9},{9,10},{10,1... | collective-permute-start | bytes 1572872 | tf_op jit(solution)/shard_map/ppermute | solution.py:728
  110.1 192.4 %collective-permute-start.1 = (bf16[1024,256]{1,0:T(8,128)(2,1)}, bf16[1024,256]{1,0:T(8,128)(2,1)}, u32[]{:S(2)}, u32[]{:S(2)}) collective-permute-start(bf16[1024,256]{1,0:T(8,128)(2,1)} %get-tuple-element.23), channel_id=1, source_target_pairs={{0,2},{1,3},{2,4},{3,5},{4,6},{5,7},{6,0},{7,1},{8,10},{9,11},{10,... | collective-permute-start | bytes 1572872 | tf_op jit(solution)/shard_map/ppermute | solution.py:728
  110.1 246.2 %collective-permute-start.2 = (bf16[1024,256]{1,0:T(8,128)(2,1)}, bf16[1024,256]{1,0:T(8,128)(2,1)}, u32[]{:S(2)}, u32[]{:S(2)}) collective-permute-start(bf16[1024,256]{1,0:T(8,128)(2,1)} %get-tuple-element.24), channel_id=1, source_target_pairs={{0,3},{1,4},{2,5},{3,6},{4,7},{5,0},{6,1},{7,2},{8,11},{9,12},{10,... | collective-permute-start | bytes 1572872 | tf_op jit(solution)/shard_map/ppermute | solution.py:728
  110.1 246.2 %collective-permute-start.3 = (bf16[1024,256]{1,0:T(8,128)(2,1)}, bf16[1024,256]{1,0:T(8,128)(2,1)}, u32[]{:S(2)}, u32[]{:S(2)}) collective-permute-start(bf16[1024,256]{1,0:T(8,128)(2,1)} %get-tuple-element.25), channel_id=1, source_target_pairs={{0,4},{1,5},{2,6},{3,7},{4,0},{5,1},{6,2},{7,3},{8,12},{9,13},{10,... | collective-permute-start | bytes 1572872 | tf_op jit(solution)/shard_map/ppermute | solution.py:728
  113.9 242.5 %collective-permute-start.4 = (bf16[1024,256]{1,0:T(8,128)(2,1)}, bf16[1024,256]{1,0:T(8,128)(2,1)}, u32[]{:S(2)}, u32[]{:S(2)}) collective-permute-start(bf16[1024,256]{1,0:T(8,128)(2,1)} %get-tuple-element.26), channel_id=1, source_target_pairs={{0,5},{1,6},{2,7},{3,0},{4,1},{5,2},{6,3},{7,4},{8,13},{9,14},{10,... | collective-permute-start | bytes 1572872 | tf_op jit(solution)/shard_map/ppermute | solution.py:728
  116.7 0.6 copy-start.12
  120.8 2.2 copy-start.17
  123.0 1.0 copy-start.14
  123.0 1.6 copy-start.18
  123.0 2.3 copy-start.2
  125.3 2.2 copy-start
  127.5 77.7 %copy-start.7 = (f32[64,1]{1,0:T(8,128)}, f32[64,1]{1,0:T(8,128)S(1)}, u32[]{:S(2)}) copy-start(f32[64,1]{1,0:T(8,128)S(1)} %broadcast_in_dim.54.scale_ref) | copy-start | bytes 772
  205.2 0.8 copy-start.6
  206.0 99.3 %copy-start.10 = (bf16[128]{0:T(256)(128)(2,1)S(1)}, bf16[128]{0:T(256)(128)(2,1)}, u32[]{:S(2)}) copy-start(bf16[128]{0:T(256)(128)(2,1)} %param.41) | copy-start | bytes 772
  299.3 57.1 %collective-permute-start.5 = (bf16[1024,256]{1,0:T(8,128)(2,1)}, bf16[1024,256]{1,0:T(8,128)(2,1)S(1)}, u32[]{:S(2)}, u32[]{:S(2)}) collective-permute-start(bf16[1024,256]{1,0:T(8,128)(2,1)} %get-tuple-element.27), channel_id=1, source_target_pairs={{0,6},{1,7},{2,0},{3,1},{4,2},{5,3},{6,4},{7,5},{8,14},{9,15},{10,... | collective-permute-start | bytes 1572872 | tf_op jit(solution)/shard_map/ppermute | solution.py:728
  302.5 53.9 %collective-permute-start.6 = (bf16[1024,256]{1,0:T(8,128)(2,1)}, bf16[1024,256]{1,0:T(8,128)(2,1)S(1)}, u32[]{:S(2)}, u32[]{:S(2)}) collective-permute-start(bf16[1024,256]{1,0:T(8,128)(2,1)} %get-tuple-element.28), channel_id=1, source_target_pairs={{0,7},{1,0},{2,1},{3,2},{4,3},{5,4},{6,5},{7,6},{8,15},{9,8},{10,9... | collective-permute-start | bytes 1572872 | tf_op jit(solution)/shard_map/ppermute | solution.py:728
  302.5 53.9 %copy-start.9 = (bf16[1024,256]{1,0:T(8,128)(2,1)S(1)}, bf16[1024,256]{1,0:T(8,128)(2,1)}, u32[]{:S(2)}) copy-start(bf16[1024,256]{1,0:T(8,128)(2,1)} %get-tuple-element.21.refs_0_) | copy-start | bytes 1572868
  305.3 1.0 copy-start.3
  306.4 2.2 copy-start.8
  356.4 41.4 %copy-start.1 = (bf16[512,4096]{1,0:T(8,128)(2,1)S(1)}, bf16[512,4096]{1,0:T(8,128)(2,1)}, u32[]{:S(2)}) copy-start(bf16[512,4096]{1,0:T(8,128)(2,1)} %wo_hbm.3) | copy-start | bytes 12582916
  356.4 41.4 %copy-start.4 = (bf16[64,4096]{1,0:T(8,128)(2,1)S(1)}, bf16[64,4096]{1,0:T(8,128)(2,1)}, u32[]{:S(2)}) copy-start(bf16[64,4096]{1,0:T(8,128)(2,1)} %shard_map.244.h_ref) | copy-start | bytes 1572868
  436.0 0.8 copy-start.5
